TPU v7x, 32 devices: a whole 2x2x4 slice. The times are simulated.
32 devices in a mesh: tp: 4 (over z), cp: 8 (over y, x, core).
Axes of the slice: x: 2, y: 2, z: 4, core: 2. Of those that a mesh axis runs over, the one named last changes fastest.
Arguments:
- q_raw: bfloat16 [4096, 16, 128], P('cp', 'tp'), parts along dimension 1
- k_raw: bfloat16 [4096, 8, 128], P('cp', 'tp'), parts along dimension 1
- v_raw: bfloat16 [4096, 8, 128], P('cp', 'tp'), parts along dimension 1
- positions: int32 [4096], P('cp')
- seq_ids: int32 [4096], P('cp')
- q_gain: bfloat16 [128], replicated
- k_gain: bfloat16 [128], replicated
Outputs:
- output 1: bfloat16 [4096, 16, 128], P('cp', 'tp'), parts along dimension 1
- output 2: float32 [4096, 16], P('cp', 'tp'), parts along dimension 1
There are 4 independent parts. A program takes and returns all parts, laid end to end along the dimension named above; an argument that names none is the same for every part.
All inputs are finite; a program needn't handle non-finite values.
Results may differ from a plain program's by a relative error of at most 0.017719.
Values are sent between devices in bfloat16 or wider.
A program may use at most 1 GiB of HBM per device.

v0:
```python
import jax
import jax.numpy as jnp
from jax import lax
from jax.sharding import PartitionSpec as P

THETA = 1000000.0
EPS = 1e-6
NEG_BIG = -1e30


def norm_rope(x_in, gain, positions):
    head_dim = x_in.shape[-1]
    half = head_dim // 2
    x_f32 = x_in.astype(jnp.float32)
    inv_rms = lax.rsqrt(jnp.mean(x_f32 * x_f32, axis=-1, keepdims=True) + EPS)
    normed = (x_f32 * inv_rms * gain.astype(jnp.float32)).astype(jnp.bfloat16).astype(jnp.float32)
    inv_freq = jnp.power(THETA, -(jnp.arange(half, dtype=jnp.float32) * 2.0) / head_dim)
    angle = positions.astype(jnp.float32)[:, None] * inv_freq[None, :]
    cos_a = jnp.cos(angle)[:, None, :]
    sin_a = jnp.sin(angle)[:, None, :]
    first = normed[..., :half]
    second = normed[..., half:]
    rotated = jnp.concatenate([first * cos_a - second * sin_a, second * cos_a + first * sin_a], axis=-1)
    return rotated.astype(jnp.bfloat16)


def key_step(stats, q_grp, q_pos, q_seq, k_blk, v_blk, k_pos, k_seq):
    max_run, sum_run, acc_run = stats
    scale = q_grp.shape[-1] ** -0.5
    scores = jnp.einsum("rkgd,skd->rkgs", q_grp, k_blk, preferred_element_type=jnp.float32) * scale
    allowed = (q_seq[:, None] == k_seq[None, :]) & (k_pos[None, :] <= q_pos[:, None])
    scores = jnp.where(allowed[:, None, None, :], scores, NEG_BIG)
    max_new = jnp.maximum(max_run, jnp.max(scores, axis=-1))
    rescale = jnp.exp(max_run - max_new)
    weights = jnp.exp(scores - max_new[..., None])
    sum_new = sum_run * rescale + jnp.sum(weights, axis=-1)
    acc_new = acc_run * rescale[..., None] + jnp.einsum("rkgs,skd->rkgd", weights.astype(jnp.bfloat16), v_blk, preferred_element_type=jnp.float32)
    return max_new, sum_new, acc_new


def solution(mesh):
    cp_size = mesh.shape["cp"]
    shift = [(src, (src + 1) % cp_size) for src in range(cp_size)]

    def per_device(q_raw, k_raw, v_raw, positions, seq_ids, q_gain, k_gain):
        rows, q_heads, head_dim = q_raw.shape
        kv_heads = k_raw.shape[1]
        group = q_heads // kv_heads
        q_grp = norm_rope(q_raw, q_gain, positions).reshape(rows, kv_heads, group, head_dim)
        k_rot = norm_rope(k_raw, k_gain, positions)
        start_stats = (jnp.full((rows, kv_heads, group), NEG_BIG, jnp.float32), jnp.zeros((rows, kv_heads, group), jnp.float32), jnp.zeros((rows, kv_heads, group, head_dim), jnp.float32))
        stats = key_step(start_stats, q_grp, positions, seq_ids, k_rot, v_raw, positions, seq_ids)

        def body(step_idx, carry):
            k_blk, v_blk, k_pos, k_seq, run_stats = carry
            k_blk = lax.ppermute(k_blk, "cp", shift)
            v_blk = lax.ppermute(v_blk, "cp", shift)
            k_pos = lax.ppermute(k_pos, "cp", shift)
            k_seq = lax.ppermute(k_seq, "cp", shift)
            run_stats = key_step(run_stats, q_grp, positions, seq_ids, k_blk, v_blk, k_pos, k_seq)
            return (k_blk, v_blk, k_pos, k_seq, run_stats)

        carry = lax.fori_loop(1, cp_size, body, (k_rot, v_raw, positions, seq_ids, stats))
        max_run, sum_run, acc_run = carry[4]
        attn_out = (acc_run / sum_run[..., None]).astype(jnp.bfloat16).reshape(rows, q_heads, head_dim)
        log_sum_exp = (max_run + jnp.log(sum_run)).reshape(rows, q_heads)
        return attn_out, log_sum_exp

    return jax.shard_map(per_device, mesh=mesh, in_specs=(P("cp", "tp", None), P("cp", "tp", None), P("cp", "tp", None), P("cp"), P("cp"), P(), P()), out_specs=(P("cp", "tp", None), P("cp", "tp")), check_vma=False)
```

profile of v0, /device:TPU:0, one launch (start us, length us, event | category | flops | bytes accessed | tf_op | source)
XLA Modules:
  0.0 94.6 jit_solution(11703296011015163735)
XLA Ops:
  2.3 1.7 %fusion.35 = f32[512,4]{1,0:T(8,128)S(1)} fusion(bf16[512,4,128]{2,1,0:T(4,128)(2,1)} %param.9), kind=kLoop, calls=%fused_computation.34 | loop fusion | flops 784384 | bytes 532480 | tf_op jit(solution)/shard_map/reduce_sum | solution.py:15
  4.7 1.7 %fusion.41 = f32[512,4,128]{2,1,0:T(4,128)S(1)} fusion(bf16[512,4,128]{2,1,0:T(4,128)(2,1)} %param.9, f32[128]{0:T(128)S(1)} %convert_element_type.46, f32[512,4]{1,0:T(8,128)S(1)} %add_rsqrt_fusion), kind=kLoop, calls=%fused_computation.46 | loop fusion | flops 1310720 | bytes 1581568 | tf_op jit(solution)/shard_map/convert_element_type | solution.py:16
  12.4 79.9 %while.22 = (s32[]{:T(128)}, bf16[512,2,128]{2,0,1:T(8,128)(2,1)S(1)}, bf16[512,2,128]{2,0,1:T(8,128)(2,1)S(1)}, s32[512]{0:T(512)S(1)}, s32[512]{0:T(512)S(1)},...) while((s32[]{:T(128)}, ...), condition=%wide.region_7.8_spmd, body=%wide.region_4.7_spmd.sunk | while | flops 549720064 | bytes 20087060 | solution.py:63
  12.9 2.6 %collective-permute-start.2 = (s32[512]{0:T(512)S(1)}, s32[512]{0:T(512)S(1)}, u32[]{:S(2)}, u32[]{:S(2)}) collective-permute-start(s32[512]{0:T(512)S(1)} %get-tuple-element.223), channel_id=1, source_target_pairs={{0,1},{1,2},{2,3},{3,4},{4,5},{5,6},{6,7},{7,0},{8,9},{9,10},{10,1... | collective-permute-start | bytes 6152 | tf_op jit(solution)/shard_map/while/body/eval_jaxpr/ppermute | solution.py:58
  17.2 2.7 %collective-permute-done.2 = s32[512]{0:T(512)S(1)} collective-permute-done((s32[512]{0:T(512)S(1)}, s32[512]{0:T(512)S(1)}, u32[]{:S(2)}, u32[]{:S(2)}) %collective-permute-start.2) | collective-permute-done | bytes 2080 | tf_op jit(solution)/shard_map/while/body/eval_jaxpr/ppermute | solution.py:58
  22.8 1.7 %fusion.62 = f32[512,2,2,128]{3,0,2,1:T(8,128)S(1)} fusion(f32[2,512,512,2]{2,1,3,0:T(8,128)S(1)} %get-tuple-element.205, f32[512,2,2]{0,2,1:T(2,128)S(1)} %max.4, pred[512,512]{0,1:T(8,128)(4,1)S(1)} %compare_and_fusion.3, f32[512,2,2,128]{3,0,2,1:T(8,128)S(1)} %get-tuple-element.227, f32[512,2,2]{0,2,1:T(2,128)S(1)} %get-tuple-element.207, ...), kind=kOutput, calls=%fused_computation.11.clone.1 | convolution fusion | flops 273154048 | bytes 6832128 | tf_op jit(solution)/shard_map/while/body/eval_jaxpr/rkgs,skd->rkgd/dot_general | solution.py:37
  26.0 2.4 %collective-permute-start.1 = (bf16[512,2,128]{2,0,1:T(8,128)(2,1)S(1)}, bf16[512,2,128]{2,0,1:T(8,128)(2,1)S(1)}, u32[]{:S(2)}, u32[]{:S(2)}) collective-permute-start(bf16[512,2,128]{2,0,1:T(8,128)(2,1)S(1)} %get-tuple-element.222), channel_id=1, source_target_pairs={{0,1},{1,2},{2,3},{3,4},{4,5},{5,6},{6,7},{7,0},{8,9},{9,10},{10,1... | collective-permute-start | bytes 786440 | tf_op jit(solution)/shard_map/while/body/eval_jaxpr/ppermute | solution.py:57
  28.5 2.7 %collective-permute-done.2 = s32[512]{0:T(512)S(1)} collective-permute-done((s32[512]{0:T(512)S(1)}, s32[512]{0:T(512)S(1)}, u32[]{:S(2)}, u32[]{:S(2)}) %collective-permute-start.2) | collective-permute-done | bytes 2080 | tf_op jit(solution)/shard_map/while/body/eval_jaxpr/ppermute | solution.py:58
  34.1 1.7 %fusion.62 = f32[512,2,2,128]{3,0,2,1:T(8,128)S(1)} fusion(f32[2,512,512,2]{2,1,3,0:T(8,128)S(1)} %get-tuple-element.205, f32[512,2,2]{0,2,1:T(2,128)S(1)} %max.4, pred[512,512]{0,1:T(8,128)(4,1)S(1)} %compare_and_fusion.3, f32[512,2,2,128]{3,0,2,1:T(8,128)S(1)} %get-tuple-element.227, f32[512,2,2]{0,2,1:T(2,128)S(1)} %get-tuple-element.207, ...), kind=kOutput, calls=%fused_computation.11.clone.1 | convolution fusion | flops 273154048 | bytes 6832128 | tf_op jit(solution)/shard_map/while/body/eval_jaxpr/rkgs,skd->rkgd/dot_general | solution.py:37
  36.4 3.3 %collective-permute-start.1 = (bf16[512,2,128]{2,0,1:T(8,128)(2,1)S(1)}, bf16[512,2,128]{2,0,1:T(8,128)(2,1)S(1)}, u32[]{:S(2)}, u32[]{:S(2)}) collective-permute-start(bf16[512,2,128]{2,0,1:T(8,128)(2,1)S(1)} %get-tuple-element.222), channel_id=1, source_target_pairs={{0,1},{1,2},{2,3},{3,4},{4,5},{5,6},{6,7},{7,0},{8,9},{9,10},{10,1... | collective-permute-start | bytes 786440 | tf_op jit(solution)/shard_map/while/body/eval_jaxpr/ppermute | solution.py:57
  39.8 2.7 %collective-permute-done.2 = s32[512]{0:T(512)S(1)} collective-permute-done((s32[512]{0:T(512)S(1)}, s32[512]{0:T(512)S(1)}, u32[]{:S(2)}, u32[]{:S(2)}) %collective-permute-start.2) | collective-permute-done | bytes 2080 | tf_op jit(solution)/shard_map/while/body/eval_jaxpr/ppermute | solution.py:58
  45.4 1.7 %fusion.62 = f32[512,2,2,128]{3,0,2,1:T(8,128)S(1)} fusion(f32[2,512,512,2]{2,1,3,0:T(8,128)S(1)} %get-tuple-element.205, f32[512,2,2]{0,2,1:T(2,128)S(1)} %max.4, pred[512,512]{0,1:T(8,128)(4,1)S(1)} %compare_and_fusion.3, f32[512,2,2,128]{3,0,2,1:T(8,128)S(1)} %get-tuple-element.227, f32[512,2,2]{0,2,1:T(2,128)S(1)} %get-tuple-element.207, ...), kind=kOutput, calls=%fused_computation.11.clone.1 | convolution fusion | flops 273154048 | bytes 6832128 | tf_op jit(solution)/shard_map/while/body/eval_jaxpr/rkgs,skd->rkgd/dot_general | solution.py:37
  47.7 3.4 %collective-permute-start.1 = (bf16[512,2,128]{2,0,1:T(8,128)(2,1)S(1)}, bf16[512,2,128]{2,0,1:T(8,128)(2,1)S(1)}, u32[]{:S(2)}, u32[]{:S(2)}) collective-permute-start(bf16[512,2,128]{2,0,1:T(8,128)(2,1)S(1)} %get-tuple-element.222), channel_id=1, source_target_pairs={{0,1},{1,2},{2,3},{3,4},{4,5},{5,6},{6,7},{7,0},{8,9},{9,10},{10,1... | collective-permute-start | bytes 786440 | tf_op jit(solution)/shard_map/while/body/eval_jaxpr/ppermute | solution.py:57
  51.1 2.7 %collective-permute-done.2 = s32[512]{0:T(512)S(1)} collective-permute-done((s32[512]{0:T(512)S(1)}, s32[512]{0:T(512)S(1)}, u32[]{:S(2)}, u32[]{:S(2)}) %collective-permute-start.2) | collective-permute-done | bytes 2080 | tf_op jit(solution)/shard_map/while/body/eval_jaxpr/ppermute | solution.py:58
  56.7 1.7 %fusion.62 = f32[512,2,2,128]{3,0,2,1:T(8,128)S(1)} fusion(f32[2,512,512,2]{2,1,3,0:T(8,128)S(1)} %get-tuple-element.205, f32[512,2,2]{0,2,1:T(2,128)S(1)} %max.4, pred[512,512]{0,1:T(8,128)(4,1)S(1)} %compare_and_fusion.3, f32[512,2,2,128]{3,0,2,1:T(8,128)S(1)} %get-tuple-element.227, f32[512,2,2]{0,2,1:T(2,128)S(1)} %get-tuple-element.207, ...), kind=kOutput, calls=%fused_computation.11.clone.1 | convolution fusion | flops 273154048 | bytes 6832128 | tf_op jit(solution)/shard_map/while/body/eval_jaxpr/rkgs,skd->rkgd/dot_general | solution.py:37
  59.0 3.4 %collective-permute-start.1 = (bf16[512,2,128]{2,0,1:T(8,128)(2,1)S(1)}, bf16[512,2,128]{2,0,1:T(8,128)(2,1)S(1)}, u32[]{:S(2)}, u32[]{:S(2)}) collective-permute-start(bf16[512,2,128]{2,0,1:T(8,128)(2,1)S(1)} %get-tuple-element.222), channel_id=1, source_target_pairs={{0,1},{1,2},{2,3},{3,4},{4,5},{5,6},{6,7},{7,0},{8,9},{9,10},{10,1... | collective-permute-start | bytes 786440 | tf_op jit(solution)/shard_map/while/body/eval_jaxpr/ppermute | solution.py:57
  62.4 2.7 %collective-permute-done.2 = s32[512]{0:T(512)S(1)} collective-permute-done((s32[512]{0:T(512)S(1)}, s32[512]{0:T(512)S(1)}, u32[]{:S(2)}, u32[]{:S(2)}) %collective-permute-start.2) | collective-permute-done | bytes 2080 | tf_op jit(solution)/shard_map/while/body/eval_jaxpr/ppermute | solution.py:58
  68.0 1.7 %fusion.62 = f32[512,2,2,128]{3,0,2,1:T(8,128)S(1)} fusion(f32[2,512,512,2]{2,1,3,0:T(8,128)S(1)} %get-tuple-element.205, f32[512,2,2]{0,2,1:T(2,128)S(1)} %max.4, pred[512,512]{0,1:T(8,128)(4,1)S(1)} %compare_and_fusion.3, f32[512,2,2,128]{3,0,2,1:T(8,128)S(1)} %get-tuple-element.227, f32[512,2,2]{0,2,1:T(2,128)S(1)} %get-tuple-element.207, ...), kind=kOutput, calls=%fused_computation.11.clone.1 | convolution fusion | flops 273154048 | bytes 6832128 | tf_op jit(solution)/shard_map/while/body/eval_jaxpr/rkgs,skd->rkgd/dot_general | solution.py:37
  70.3 3.4 %collective-permute-start.1 = (bf16[512,2,128]{2,0,1:T(8,128)(2,1)S(1)}, bf16[512,2,128]{2,0,1:T(8,128)(2,1)S(1)}, u32[]{:S(2)}, u32[]{:S(2)}) collective-permute-start(bf16[512,2,128]{2,0,1:T(8,128)(2,1)S(1)} %get-tuple-element.222), channel_id=1, source_target_pairs={{0,1},{1,2},{2,3},{3,4},{4,5},{5,6},{6,7},{7,0},{8,9},{9,10},{10,1... | collective-permute-start | bytes 786440 | tf_op jit(solution)/shard_map/while/body/eval_jaxpr/ppermute | solution.py:57
  73.7 2.7 %collective-permute-done.2 = s32[512]{0:T(512)S(1)} collective-permute-done((s32[512]{0:T(512)S(1)}, s32[512]{0:T(512)S(1)}, u32[]{:S(2)}, u32[]{:S(2)}) %collective-permute-start.2) | collective-permute-done | bytes 2080 | tf_op jit(solution)/shard_map/while/body/eval_jaxpr/ppermute | solution.py:58
  79.3 1.7 %fusion.62 = f32[512,2,2,128]{3,0,2,1:T(8,128)S(1)} fusion(f32[2,512,512,2]{2,1,3,0:T(8,128)S(1)} %get-tuple-element.205, f32[512,2,2]{0,2,1:T(2,128)S(1)} %max.4, pred[512,512]{0,1:T(8,128)(4,1)S(1)} %compare_and_fusion.3, f32[512,2,2,128]{3,0,2,1:T(8,128)S(1)} %get-tuple-element.227, f32[512,2,2]{0,2,1:T(2,128)S(1)} %get-tuple-element.207, ...), kind=kOutput, calls=%fused_computation.11.clone.1 | convolution fusion | flops 273154048 | bytes 6832128 | tf_op jit(solution)/shard_map/while/body/eval_jaxpr/rkgs,skd->rkgd/dot_general | solution.py:37
  81.6 3.4 %collective-permute-start.1 = (bf16[512,2,128]{2,0,1:T(8,128)(2,1)S(1)}, bf16[512,2,128]{2,0,1:T(8,128)(2,1)S(1)}, u32[]{:S(2)}, u32[]{:S(2)}) collective-permute-start(bf16[512,2,128]{2,0,1:T(8,128)(2,1)S(1)} %get-tuple-element.222), channel_id=1, source_target_pairs={{0,1},{1,2},{2,3},{3,4},{4,5},{5,6},{6,7},{7,0},{8,9},{9,10},{10,1... | collective-permute-start | bytes 786440 | tf_op jit(solution)/shard_map/while/body/eval_jaxpr/ppermute | solution.py:57
  85.0 2.7 %collective-permute-done.2 = s32[512]{0:T(512)S(1)} collective-permute-done((s32[512]{0:T(512)S(1)}, s32[512]{0:T(512)S(1)}, u32[]{:S(2)}, u32[]{:S(2)}) %collective-permute-start.2) | collective-permute-done | bytes 2080 | tf_op jit(solution)/shard_map/while/body/eval_jaxpr/ppermute | solution.py:58
  90.6 1.7 %fusion.62 = f32[512,2,2,128]{3,0,2,1:T(8,128)S(1)} fusion(f32[2,512,512,2]{2,1,3,0:T(8,128)S(1)} %get-tuple-element.205, f32[512,2,2]{0,2,1:T(2,128)S(1)} %max.4, pred[512,512]{0,1:T(8,128)(4,1)S(1)} %compare_and_fusion.3, f32[512,2,2,128]{3,0,2,1:T(8,128)S(1)} %get-tuple-element.227, f32[512,2,2]{0,2,1:T(2,128)S(1)} %get-tuple-element.207, ...), kind=kOutput, calls=%fused_computation.11.clone.1 | convolution fusion | flops 273154048 | bytes 6832128 | tf_op jit(solution)/shard_map/while/body/eval_jaxpr/rkgs,skd->rkgd/dot_general | solution.py:37
  (150 shorter events, 36.9 us)
Async XLA Ops:
  12.4 7.8 %collective-permute-start = (bf16[512,2,128]{2,0,1:T(8,128)(2,1)S(1)}, bf16[512,2,128]{2,0,1:T(8,128)(2,1)S(1)}, u32[]{:S(2)}, u32[]{:S(2)}) collective-permute-start(bf16[512,2,128]{2,0,1:T(8,128)(2,1)S(1)} %get-tuple-element.221), channel_id=1, source_target_pairs={{0,1},{1,2},{2,3},{3,4},{4,5},{5,6},{6,7},{7,0},{8,9},{9,10},{10,1... | collective-permute-start | bytes 786440 | tf_op jit(solution)/shard_map/while/body/eval_jaxpr/ppermute | solution.py:56
  12.9 7.0 %collective-permute-start.2 = (s32[512]{0:T(512)S(1)}, s32[512]{0:T(512)S(1)}, u32[]{:S(2)}, u32[]{:S(2)}) collective-permute-start(s32[512]{0:T(512)S(1)} %get-tuple-element.223), channel_id=1, source_target_pairs={{0,1},{1,2},{2,3},{3,4},{4,5},{5,6},{6,7},{7,0},{8,9},{9,10},{10,1... | collective-permute-start | bytes 6152 | tf_op jit(solution)/shard_map/while/body/eval_jaxpr/ppermute | solution.py:58
  15.6 7.1 %collective-permute-start.1 = (bf16[512,2,128]{2,0,1:T(8,128)(2,1)S(1)}, bf16[512,2,128]{2,0,1:T(8,128)(2,1)S(1)}, u32[]{:S(2)}, u32[]{:S(2)}) collective-permute-start(bf16[512,2,128]{2,0,1:T(8,128)(2,1)S(1)} %get-tuple-element.222), channel_id=1, source_target_pairs={{0,1},{1,2},{2,3},{3,4},{4,5},{5,6},{6,7},{7,0},{8,9},{9,10},{10,1... | collective-permute-start | bytes 786440 | tf_op jit(solution)/shard_map/while/body/eval_jaxpr/ppermute | solution.py:57
  24.4 7.1 %collective-permute-start = (bf16[512,2,128]{2,0,1:T(8,128)(2,1)S(1)}, bf16[512,2,128]{2,0,1:T(8,128)(2,1)S(1)}, u32[]{:S(2)}, u32[]{:S(2)}) collective-permute-start(bf16[512,2,128]{2,0,1:T(8,128)(2,1)S(1)} %get-tuple-element.221), channel_id=1, source_target_pairs={{0,1},{1,2},{2,3},{3,4},{4,5},{5,6},{6,7},{7,0},{8,9},{9,10},{10,1... | collective-permute-start | bytes 786440 | tf_op jit(solution)/shard_map/while/body/eval_jaxpr/ppermute | solution.py:56
  24.5 6.7 %collective-permute-start.2 = (s32[512]{0:T(512)S(1)}, s32[512]{0:T(512)S(1)}, u32[]{:S(2)}, u32[]{:S(2)}) collective-permute-start(s32[512]{0:T(512)S(1)} %get-tuple-element.223), channel_id=1, source_target_pairs={{0,1},{1,2},{2,3},{3,4},{4,5},{5,6},{6,7},{7,0},{8,9},{9,10},{10,1... | collective-permute-start | bytes 6152 | tf_op jit(solution)/shard_map/while/body/eval_jaxpr/ppermute | solution.py:58
  26.0 8.0 %collective-permute-start.1 = (bf16[512,2,128]{2,0,1:T(8,128)(2,1)S(1)}, bf16[512,2,128]{2,0,1:T(8,128)(2,1)S(1)}, u32[]{:S(2)}, u32[]{:S(2)}) collective-permute-start(bf16[512,2,128]{2,0,1:T(8,128)(2,1)S(1)} %get-tuple-element.222), channel_id=1, source_target_pairs={{0,1},{1,2},{2,3},{3,4},{4,5},{5,6},{6,7},{7,0},{8,9},{9,10},{10,1... | collective-permute-start | bytes 786440 | tf_op jit(solution)/shard_map/while/body/eval_jaxpr/ppermute | solution.py:57
  35.8 7.1 %collective-permute-start = (bf16[512,2,128]{2,0,1:T(8,128)(2,1)S(1)}, bf16[512,2,128]{2,0,1:T(8,128)(2,1)S(1)}, u32[]{:S(2)}, u32[]{:S(2)}) collective-permute-start(bf16[512,2,128]{2,0,1:T(8,128)(2,1)S(1)} %get-tuple-element.221), channel_id=1, source_target_pairs={{0,1},{1,2},{2,3},{3,4},{4,5},{5,6},{6,7},{7,0},{8,9},{9,10},{10,1... | collective-permute-start | bytes 786440 | tf_op jit(solution)/shard_map/while/body/eval_jaxpr/ppermute | solution.py:56
  35.8 6.7 %collective-permute-start.2 = (s32[512]{0:T(512)S(1)}, s32[512]{0:T(512)S(1)}, u32[]{:S(2)}, u32[]{:S(2)}) collective-permute-start(s32[512]{0:T(512)S(1)} %get-tuple-element.223), channel_id=1, source_target_pairs={{0,1},{1,2},{2,3},{3,4},{4,5},{5,6},{6,7},{7,0},{8,9},{9,10},{10,1... | collective-permute-start | bytes 6152 | tf_op jit(solution)/shard_map/while/body/eval_jaxpr/ppermute | solution.py:58
  36.4 8.9 %collective-permute-start.1 = (bf16[512,2,128]{2,0,1:T(8,128)(2,1)S(1)}, bf16[512,2,128]{2,0,1:T(8,128)(2,1)S(1)}, u32[]{:S(2)}, u32[]{:S(2)}) collective-permute-start(bf16[512,2,128]{2,0,1:T(8,128)(2,1)S(1)} %get-tuple-element.222), channel_id=1, source_target_pairs={{0,1},{1,2},{2,3},{3,4},{4,5},{5,6},{6,7},{7,0},{8,9},{9,10},{10,1... | collective-permute-start | bytes 786440 | tf_op jit(solution)/shard_map/while/body/eval_jaxpr/ppermute | solution.py:57
  47.1 7.1 %collective-permute-start = (bf16[512,2,128]{2,0,1:T(8,128)(2,1)S(1)}, bf16[512,2,128]{2,0,1:T(8,128)(2,1)S(1)}, u32[]{:S(2)}, u32[]{:S(2)}) collective-permute-start(bf16[512,2,128]{2,0,1:T(8,128)(2,1)S(1)} %get-tuple-element.221), channel_id=1, source_target_pairs={{0,1},{1,2},{2,3},{3,4},{4,5},{5,6},{6,7},{7,0},{8,9},{9,10},{10,1... | collective-permute-start | bytes 786440 | tf_op jit(solution)/shard_map/while/body/eval_jaxpr/ppermute | solution.py:56
  47.1 6.7 %collective-permute-start.2 = (s32[512]{0:T(512)S(1)}, s32[512]{0:T(512)S(1)}, u32[]{:S(2)}, u32[]{:S(2)}) collective-permute-start(s32[512]{0:T(512)S(1)} %get-tuple-element.223), channel_id=1, source_target_pairs={{0,1},{1,2},{2,3},{3,4},{4,5},{5,6},{6,7},{7,0},{8,9},{9,10},{10,1... | collective-permute-start | bytes 6152 | tf_op jit(solution)/shard_map/while/body/eval_jaxpr/ppermute | solution.py:58
  47.4 6.5 %collective-permute-start.3 = (s32[512]{0:T(512)S(1)}, s32[512]{0:T(512)S(1)}, u32[]{:S(2)}, u32[]{:S(2)}) collective-permute-start(s32[512]{0:T(512)S(1)} %get-tuple-element.224), channel_id=1, source_target_pairs={{0,1},{1,2},{2,3},{3,4},{4,5},{5,6},{6,7},{7,0},{8,9},{9,10},{10,1... | collective-permute-start | bytes 6152 | tf_op jit(solution)/shard_map/while/body/eval_jaxpr/ppermute | solution.py:59
  47.7 9.0 %collective-permute-start.1 = (bf16[512,2,128]{2,0,1:T(8,128)(2,1)S(1)}, bf16[512,2,128]{2,0,1:T(8,128)(2,1)S(1)}, u32[]{:S(2)}, u32[]{:S(2)}) collective-permute-start(bf16[512,2,128]{2,0,1:T(8,128)(2,1)S(1)} %get-tuple-element.222), channel_id=1, source_target_pairs={{0,1},{1,2},{2,3},{3,4},{4,5},{5,6},{6,7},{7,0},{8,9},{9,10},{10,1... | collective-permute-start | bytes 786440 | tf_op jit(solution)/shard_map/while/body/eval_jaxpr/ppermute | solution.py:57
  58.4 7.1 %collective-permute-start = (bf16[512,2,128]{2,0,1:T(8,128)(2,1)S(1)}, bf16[512,2,128]{2,0,1:T(8,128)(2,1)S(1)}, u32[]{:S(2)}, u32[]{:S(2)}) collective-permute-start(bf16[512,2,128]{2,0,1:T(8,128)(2,1)S(1)} %get-tuple-element.221), channel_id=1, source_target_pairs={{0,1},{1,2},{2,3},{3,4},{4,5},{5,6},{6,7},{7,0},{8,9},{9,10},{10,1... | collective-permute-start | bytes 786440 | tf_op jit(solution)/shard_map/while/body/eval_jaxpr/ppermute | solution.py:56
  58.4 6.7 %collective-permute-start.2 = (s32[512]{0:T(512)S(1)}, s32[512]{0:T(512)S(1)}, u32[]{:S(2)}, u32[]{:S(2)}) collective-permute-start(s32[512]{0:T(512)S(1)} %get-tuple-element.223), channel_id=1, source_target_pairs={{0,1},{1,2},{2,3},{3,4},{4,5},{5,6},{6,7},{7,0},{8,9},{9,10},{10,1... | collective-permute-start | bytes 6152 | tf_op jit(solution)/shard_map/while/body/eval_jaxpr/ppermute | solution.py:58
  58.7 6.5 %collective-permute-start.3 = (s32[512]{0:T(512)S(1)}, s32[512]{0:T(512)S(1)}, u32[]{:S(2)}, u32[]{:S(2)}) collective-permute-start(s32[512]{0:T(512)S(1)} %get-tuple-element.224), channel_id=1, source_target_pairs={{0,1},{1,2},{2,3},{3,4},{4,5},{5,6},{6,7},{7,0},{8,9},{9,10},{10,1... | collective-permute-start | bytes 6152 | tf_op jit(solution)/shard_map/while/body/eval_jaxpr/ppermute | solution.py:59
  59.0 9.0 %collective-permute-start.1 = (bf16[512,2,128]{2,0,1:T(8,128)(2,1)S(1)}, bf16[512,2,128]{2,0,1:T(8,128)(2,1)S(1)}, u32[]{:S(2)}, u32[]{:S(2)}) collective-permute-start(bf16[512,2,128]{2,0,1:T(8,128)(2,1)S(1)} %get-tuple-element.222), channel_id=1, source_target_pairs={{0,1},{1,2},{2,3},{3,4},{4,5},{5,6},{6,7},{7,0},{8,9},{9,10},{10,1... | collective-permute-start | bytes 786440 | tf_op jit(solution)/shard_map/while/body/eval_jaxpr/ppermute | solution.py:57
  69.7 7.1 %collective-permute-start = (bf16[512,2,128]{2,0,1:T(8,128)(2,1)S(1)}, bf16[512,2,128]{2,0,1:T(8,128)(2,1)S(1)}, u32[]{:S(2)}, u32[]{:S(2)}) collective-permute-start(bf16[512,2,128]{2,0,1:T(8,128)(2,1)S(1)} %get-tuple-element.221), channel_id=1, source_target_pairs={{0,1},{1,2},{2,3},{3,4},{4,5},{5,6},{6,7},{7,0},{8,9},{9,10},{10,1... | collective-permute-start | bytes 786440 | tf_op jit(solution)/shard_map/while/body/eval_jaxpr/ppermute | solution.py:56
  69.7 6.7 %collective-permute-start.2 = (s32[512]{0:T(512)S(1)}, s32[512]{0:T(512)S(1)}, u32[]{:S(2)}, u32[]{:S(2)}) collective-permute-start(s32[512]{0:T(512)S(1)} %get-tuple-element.223), channel_id=1, source_target_pairs={{0,1},{1,2},{2,3},{3,4},{4,5},{5,6},{6,7},{7,0},{8,9},{9,10},{10,1... | collective-permute-start | bytes 6152 | tf_op jit(solution)/shard_map/while/body/eval_jaxpr/ppermute | solution.py:58
  70.0 6.5 %collective-permute-start.3 = (s32[512]{0:T(512)S(1)}, s32[512]{0:T(512)S(1)}, u32[]{:S(2)}, u32[]{:S(2)}) collective-permute-start(s32[512]{0:T(512)S(1)} %get-tuple-element.224), channel_id=1, source_target_pairs={{0,1},{1,2},{2,3},{3,4},{4,5},{5,6},{6,7},{7,0},{8,9},{9,10},{10,1... | collective-permute-start | bytes 6152 | tf_op jit(solution)/shard_map/while/body/eval_jaxpr/ppermute | solution.py:59
  70.3 9.0 %collective-permute-start.1 = (bf16[512,2,128]{2,0,1:T(8,128)(2,1)S(1)}, bf16[512,2,128]{2,0,1:T(8,128)(2,1)S(1)}, u32[]{:S(2)}, u32[]{:S(2)}) collective-permute-start(bf16[512,2,128]{2,0,1:T(8,128)(2,1)S(1)} %get-tuple-element.222), channel_id=1, source_target_pairs={{0,1},{1,2},{2,3},{3,4},{4,5},{5,6},{6,7},{7,0},{8,9},{9,10},{10,1... | collective-permute-start | bytes 786440 | tf_op jit(solution)/shard_map/while/body/eval_jaxpr/ppermute | solution.py:57
  81.0 7.1 %collective-permute-start = (bf16[512,2,128]{2,0,1:T(8,128)(2,1)S(1)}, bf16[512,2,128]{2,0,1:T(8,128)(2,1)S(1)}, u32[]{:S(2)}, u32[]{:S(2)}) collective-permute-start(bf16[512,2,128]{2,0,1:T(8,128)(2,1)S(1)} %get-tuple-element.221), channel_id=1, source_target_pairs={{0,1},{1,2},{2,3},{3,4},{4,5},{5,6},{6,7},{7,0},{8,9},{9,10},{10,1... | collective-permute-start | bytes 786440 | tf_op jit(solution)/shard_map/while/body/eval_jaxpr/ppermute | solution.py:56
  81.0 6.7 %collective-permute-start.2 = (s32[512]{0:T(512)S(1)}, s32[512]{0:T(512)S(1)}, u32[]{:S(2)}, u32[]{:S(2)}) collective-permute-start(s32[512]{0:T(512)S(1)} %get-tuple-element.223), channel_id=1, source_target_pairs={{0,1},{1,2},{2,3},{3,4},{4,5},{5,6},{6,7},{7,0},{8,9},{9,10},{10,1... | collective-permute-start | bytes 6152 | tf_op jit(solution)/shard_map/while/body/eval_jaxpr/ppermute | solution.py:58
  81.6 9.0 %collective-permute-start.1 = (bf16[512,2,128]{2,0,1:T(8,128)(2,1)S(1)}, bf16[512,2,128]{2,0,1:T(8,128)(2,1)S(1)}, u32[]{:S(2)}, u32[]{:S(2)}) collective-permute-start(bf16[512,2,128]{2,0,1:T(8,128)(2,1)S(1)} %get-tuple-element.222), channel_id=1, source_target_pairs={{0,1},{1,2},{2,3},{3,4},{4,5},{5,6},{6,7},{7,0},{8,9},{9,10},{10,1... | collective-permute-start | bytes 786440 | tf_op jit(solution)/shard_map/while/body/eval_jaxpr/ppermute | solution.py:57
  (9 other events, 31.6 us)
where the time goes:
time: 94.8 us; the launch traced here: 94.6 us
  starting transfers between devices  28.9 us (30%)
  waiting for transfers between devices  23.7 us (25%)
  matrix products  20.3 us (21%)
  other arithmetic  17.8 us (19%)
  local copies, waits for them, and re-layouts  2.46 us (3%)
    ppermute x7, starting transfers between devices, body(): v_blk = lax.ppermute(v_blk, 'cp', shift)  20.9 us
    ppermute x7, waiting for transfers between devices, body(): k_pos = lax.ppermute(k_pos, 'cp', shift)  19.2 us
    dot_general x8, matrix products, key_step(): jnp.einsum('rkgs,skd->rkgd', weights.astype(jnp.bfloat16), v_blk, preferr...  13.1 us
    reduce_sum x8, other arithmetic, key_step(): sum_new = sum_run * rescale + jnp.sum(weights, axis=-1)  7.27 us
    dot_general x8, matrix products, key_step(): jnp.einsum('rkgd,skd->rkgs', q_grp, k_blk, preferred_element_type=jnp.flo...  7.18 us
    ppermute x7, starting transfers between devices, body(): k_pos = lax.ppermute(k_pos, 'cp', shift)  5.69 us
    ppermute x7, waiting for transfers between devices, body(): v_blk = lax.ppermute(v_blk, 'cp', shift)  4.37 us
    and x8, other arithmetic, key_step(): (q_seq[:, None] == k_seq[None, :]) & (k_pos[None, :] <= q_pos[:, None])  2.2 us
  transfers between devices with their start and end apart: 28, of which 14 were waited for; matrix products, arithmetic and copies ran while one was open for 16% of the time, Pallas kernels for 0%

commit v1 on v0

v1 whole, which is shorter than its diff:
```python
import functools
import math

import jax
import jax.numpy as jnp
import numpy as np
from jax import lax
from jax.experimental import pallas as pl
from jax.experimental.pallas import tpu as pltpu
from jax.sharding import PartitionSpec as P

THETA = 1000000.0
EPS = 1e-6
NEG_BIG = -1e30
D = 128
HALF = 256
ROWS = 512
C_EXP = (D ** -0.5) * math.log2(math.e)
SCALE = D ** -0.5
F32 = jnp.float32
BF16 = jnp.bfloat16


def nt(a, b):
    return lax.dot_general(a, b, (((1,), (1,)), ((), ())), preferred_element_type=F32)


def nn(a, b):
    return lax.dot_general(a, b, (((1,), (0,)), ((), ())), preferred_element_type=F32)


def kernel(q_hbm, k_hbm, v_hbm, pos_hbm, seq_hbm, qg_hbm, kg_hbm, freq_hbm, out_hbm, lse_hbm,
           q_in, k_in, v_in, pos_v, seq_v, qg_v, kg_v, freq_v, f_scr, cs_scr, perm, perm_t,
           kbuf, vbuf, kst, vst, qbuf, qst, kaug, m_scr, l_scr, acc, ost, obuf, lst, lbuf, out_v, lse_v,
           in_sem, out_sem, s_kx, s_vx, s_p, s_q, s_fk, s_fv, s_o, s_l, r_k, r_v, r_q, r_o, r_l):
    me = lax.axis_index("cp")
    core = lax.rem(me, 2)
    chip = lax.div(me, 2)
    x = lax.rem(chip, 2)
    y = lax.div(chip, 2)
    xchip = chip + 1 - 2 * x
    ychip = chip + 2 - 4 * y
    other = 1 - core
    partner = 2 * chip + other

    def rcopy(src, dst, ssem, rsem, dev):
        return pltpu.make_async_remote_copy(src_ref=src, dst_ref=dst, send_sem=ssem, recv_sem=rsem,
                                            device_id={"cp": dev}, device_id_type=pl.DeviceIdType.MESH)

    ins = [(v_hbm, v_in), (seq_hbm, seq_v), (pos_hbm, pos_v), (k_hbm, k_in), (kg_hbm, kg_v), (freq_hbm, freq_v),
           (q_hbm, q_in), (qg_hbm, qg_v)]
    in_copies = [pltpu.make_async_copy(src, dst, in_sem.at[n]) for n, (src, dst) in enumerate(ins)]
    for cp in in_copies:
        cp.start()
    barrier = pltpu.get_barrier_semaphore()
    peers = [partner, 2 * xchip, 2 * xchip + 1, 2 * ychip, 2 * ychip + 1]
    for peer in peers:
        pl.semaphore_signal(barrier, inc=1, device_id={"cp": peer}, device_id_type=pl.DeviceIdType.MESH)

    in_copies[1].wait()
    seq = seq_v[...]
    row_id = lax.broadcasted_iota(jnp.int32, (8, ROWS), 1).astype(F32)
    sub_id = lax.broadcasted_iota(jnp.int32, (8, ROWS), 0)
    is_seq = jnp.broadcast_to(seq, (8, ROWS)) == sub_id
    seq_f = jnp.where(is_seq, 1.0, 0.0)
    cnt = jnp.sum(seq_f, axis=1, keepdims=True)
    start = jnp.min(jnp.where(is_seq, row_id, float(ROWS)), axis=1, keepdims=True)
    start_row = jnp.sum(seq_f * start, axis=0, keepdims=True)
    cnt_row = jnp.sum(seq_f * cnt, axis=0, keepdims=True)
    off = row_id[:1] - start_row
    late = off * 2.0 >= cnt_row
    dest = start_row * 0.5 + off + jnp.where(late, HALF - 0.5 * cnt_row, 0.0)
    dest_i = dest.astype(jnp.int32)
    for blk in range(4):
        rows = lax.broadcasted_iota(jnp.int32, (128, ROWS), 0) + blk * 128
        perm[pl.ds(blk * 128, 128), :] = jnp.where(rows == dest_i, 1.0, 0.0).astype(BF16)

    in_copies[0].wait()
    f_scr[pl.ds(0, 1024), :] = v_in[...].astype(F32)
    for h in range(2):
        vt = f_scr[pl.ds(h, ROWS, stride=2), :].T.astype(BF16)
        vc = nt(vt, perm[...]).astype(BF16)
        for half in range(2):
            vst[h, half] = vc[:, half * HALF:(half + 1) * HALF]
    for half in range(2):
        vbuf[0, half, core] = vst[core, half]
    pl.semaphore_wait(barrier, 5)

    sends = []
    for half in range(2):
        for h in range(2):
            for t, tchip in enumerate((xchip, ychip)):
                sends.append(rcopy(vst.at[h, half], vbuf.at[1 + t, half, core], s_vx.at[t, h, half],
                                   r_v.at[1 + t, core, half], 2 * tchip + h))
                sends[-1].start()
    for half in range(2):
        sends.append(rcopy(vst.at[other, half], vbuf.at[0, half, core], s_p.at[0, half], r_v.at[0, core, half], partner))
        sends[-1].start()

    in_copies[2].wait()
    in_copies[5].wait()
    angle = freq_v[...] * pos_v[...].astype(F32)
    cs_scr[0] = jnp.cos(angle)
    cs_scr[1] = jnp.sin(angle)

    def norm_rope(rows_f32, gain_v):
        xt = rows_f32.T
        inv = lax.rsqrt(jnp.mean(xt * xt, axis=0, keepdims=True) + EPS)
        gain = jnp.broadcast_to(gain_v[...].astype(F32), (128, D)).T
        gain = jnp.concatenate([gain] * 4, axis=1)
        n = (xt * inv * gain).astype(BF16).astype(F32)
        a, b = n[:64], n[64:]
        cos, sin = cs_scr[0], cs_scr[1]
        return jnp.concatenate([a * cos - b * sin, b * cos + a * sin], axis=0).astype(BF16)

    in_copies[3].wait()
    in_copies[4].wait()
    f_scr[pl.ds(0, 1024), :] = k_in[...].astype(F32)
    for h in range(2):
        kr = norm_rope(f_scr[pl.ds(h, ROWS, stride=2), :], kg_v)
        kc = nt(perm[...], kr).astype(BF16)
        for half in range(2):
            kst[h, half] = kc[half * HALF:(half + 1) * HALF, :]
    for half in range(2):
        kbuf[0, half, core] = kst[core, half]

    for half in range(2):
        for h in range(2):
            for t, tchip in enumerate((xchip, ychip)):
                sends.append(rcopy(kst.at[h, half], kbuf.at[1 + t, half, core], s_kx.at[t, h, half],
                                   r_k.at[1 + t, core, half], 2 * tchip + h))
                sends[-1].start()
    for half in range(2):
        sends.append(rcopy(kst.at[other, half], kbuf.at[0, half, core], s_p.at[1, half], r_k.at[0, core, half], partner))
        sends[-1].start()

    in_copies[6].wait()
    in_copies[7].wait()
    f_scr[...] = q_in[...].astype(F32)

    def q_head(h, store):
        qr = norm_rope(f_scr[pl.ds(h, ROWS, stride=4), :], qg_v)
        qc = nt(qr, perm[...]).astype(BF16)
        for half in range(2):
            store(half, qc[:, half * HALF:(half + 1) * HALF])

    for g in range(2):
        def store_other(half, val, g=g):
            qst[half, :, g * HALF:(g + 1) * HALF] = val
        q_head(2 * other + g, store_other)
    for half in range(2):
        sends.append(rcopy(qst.at[half], qbuf.at[half, 0, pl.ds(0, D), :], s_q.at[half], r_q.at[half], partner))
        sends[-1].start()
    for g in range(2):
        def store_own(half, val, g=g):
            qbuf[half, 1, pl.ds(0, D), g * HALF:(g + 1) * HALF] = val
        q_head(2 * core + g, store_own)

    lane_d = lax.broadcasted_iota(jnp.int32, (8, HALF), 1).astype(F32)
    in_run = (lane_d >= start * 0.5) & (lane_d < (start + cnt) * 0.5)
    one_hot = jnp.where(in_run, 1.0, 0.0)
    blocked = jnp.where(in_run, 0.0, NEG_BIG)
    blocked = jnp.where(lax.broadcasted_iota(jnp.int32, (8, HALF), 0) < 4, blocked, 0.0)
    pad = jnp.zeros((D - 8, HALF), F32)
    q_extra = jnp.concatenate([blocked, pad], axis=0).astype(BF16)
    for half in range(2):
        for dev in range(2):
            for g in range(2):
                qbuf[half, dev, pl.ds(D, D), g * HALF:(g + 1) * HALF] = q_extra
    kaug[...] = jnp.concatenate([one_hot, pad], axis=0).T.astype(BF16)

    dest_cols = jnp.broadcast_to(dest, (128, ROWS)).T.astype(jnp.int32)
    for blk in range(4):
        lanes = lax.broadcasted_iota(jnp.int32, (ROWS, 128), 1) + blk * 128
        perm_t[:, blk * 128:(blk + 1) * 128] = jnp.where(lanes == dest_cols, 1.0, 0.0).astype(BF16)

    m_scr[...] = jnp.full(m_scr.shape, NEG_BIG, F32)
    l_scr[...] = jnp.zeros(l_scr.shape, F32)
    acc[...] = jnp.zeros(acc.shape, F32)

    def tile(slot, khalf, qhalf, causal):
        keys = kbuf[slot, khalf].reshape(2 * HALF, D)
        ka = kaug[...]
        keys = jnp.concatenate([keys, jnp.concatenate([ka, ka], axis=0)], axis=1)
        v0 = vbuf[slot, khalf, 0]
        v1 = vbuf[slot, khalf, 1]
        for dev in range(2):
            for g in range(2):
                cols = pl.ds(g * HALF, HALF)
                s = nn(keys, qbuf[qhalf, dev, :, cols])
                if causal:
                    abs_dev = core if dev == 1 else other
                    krow = lax.broadcasted_iota(jnp.int32, (2 * HALF, HALF), 0)
                    qcol = lax.broadcasted_iota(jnp.int32, (2 * HALF, HALF), 1)
                    kord = krow + qhalf * jnp.where(krow < HALF, HALF, -HALF)
                    qord = qcol + (abs_dev + qhalf * (1 - 2 * abs_dev)) * HALF
                    s = jnp.where(kord <= qord, s, NEG_BIG)
                m_old = m_scr[qhalf, dev, :, cols]
                m_new = jnp.maximum(m_old, jnp.max(s, axis=0, keepdims=True))
                p = jnp.exp2((s - m_new) * C_EXP)
                alpha = jnp.exp2((m_old - m_new) * C_EXP)
                m_scr[qhalf, dev, :, cols] = m_new
                l_scr[qhalf, dev, :, cols] = l_scr[qhalf, dev, :, cols] * alpha + jnp.sum(p, axis=0, keepdims=True)
                pb = p.astype(BF16)
                o = nn(v0, pb[:HALF]) + nn(v1, pb[HALF:])
                acc[qhalf, dev, :, cols] = acc[qhalf, dev, :, cols] * alpha + o

    def got_k(slot, dev, half):
        rcopy(kst.at[0, half], kbuf.at[slot, half, dev], s_kx.at[0, 0, half], r_k.at[slot, dev, half], partner).wait_recv()

    def got_v(slot, dev, half):
        rcopy(vst.at[0, half], vbuf.at[slot, half, dev], s_vx.at[0, 0, half], r_v.at[slot, dev, half], partner).wait_recv()

    for half in range(2):
        got_v(0, other, half)
        got_k(0, other, half)
        rcopy(qst.at[half], qbuf.at[half, 0, pl.ds(0, D), :], s_q.at[half], r_q.at[half], partner).wait_recv()

    def own_body(half, carry):
        tile(0, half, half, True)
        return carry

    lax.fori_loop(0, 2, own_body, 0)

    def fwd_v(dev, half):
        return rcopy(vbuf.at[2, half, dev], vbuf.at[3, half, dev], s_fv.at[dev, half], r_v.at[3, dev, half], 2 * xchip + core)

    def fwd_k(dev, half):
        return rcopy(kbuf.at[1, half, dev], kbuf.at[3, half, dev], s_fk.at[dev, half], r_k.at[3, dev, half], 2 * ychip + core)

    def body(idx, carry):
        grp = (idx + 1) // 2
        second = (idx + 1) % 2

        @pl.when(idx == 1)
        def _():
            for half in range(2):
                for dev in range(2):
                    got_v(2, dev, half)
                    fwd_v(dev, half).start()
            for dev in range(2):
                got_k(1, dev, 0)
                fwd_k(dev, 0).start()
                got_v(1, dev, 0)

        @pl.when(idx == 2)
        def _():
            for dev in range(2):
                got_k(1, dev, 1)
                fwd_k(dev, 1).start()
                got_v(1, dev, 1)

        @pl.when(idx == 3)
        def _():
            for dev in range(2):
                got_k(2, dev, 0)

        @pl.when(idx == 4)
        def _():
            for dev in range(2):
                got_k(2, dev, 1)

        @pl.when(idx == 5)
        def _():
            for dev in range(2):
                got_v(3, dev, 0)
                got_k(3, dev, 0)

        @pl.when(idx == 6)
        def _():
            for dev in range(2):
                got_v(3, dev, 1)
                got_k(3, dev, 1)

        use_x = (4 - grp) // 3
        late_needed = (1 - y) + use_x * (y - x)
        snd = second * ((idx + 6) // 7)
        sel = snd * late_needed
        tile(grp * ((idx + 6) // 7), sel, 1 - snd + sel, False)
        return carry

    lax.fori_loop(0, 7, body, 0)

    def finish(dev, dst_o, dst_l):
        for half in range(2):
            for g in range(2):
                cols = pl.ds(g * HALF, HALF)
                l = l_scr[half, dev, :, cols]
                o = acc[half, dev, :, cols] * (1.0 / l)
                dst_o(half, g, o.astype(BF16))
                dst_l(half, g, m_scr[half, dev, :, cols] * SCALE + jnp.log(l))

    def st_o(half, g, val):
        ost[g, :, half * HALF:(half + 1) * HALF] = val

    def st_l(half, g, val):
        lst[pl.ds(g, 1), half * HALF:(half + 1) * HALF] = val

    finish(0, st_o, st_l)
    o_send = rcopy(ost, obuf.at[core], s_o.at[0], r_o.at[0], partner)
    l_send = rcopy(lst, lbuf.at[core], s_l.at[0], r_l.at[0], partner)
    o_send.start()
    l_send.start()

    def own_o(half, g, val):
        obuf[core, g, :, half * HALF:(half + 1) * HALF] = val

    def own_l(half, g, val):
        lbuf[core, pl.ds(g, 1), half * HALF:(half + 1) * HALF] = val

    finish(1, own_o, own_l)

    def place(grp):
        for g in range(2):
            f_scr[pl.ds(2 * grp + g, ROWS, stride=4), :] = nt(perm_t[...], obuf[grp, g])

    place(core)
    rcopy(ost, obuf.at[other], s_o.at[0], r_o.at[0], partner).wait_recv()
    rcopy(lst, lbuf.at[other], s_l.at[0], r_l.at[0], partner).wait_recv()
    place(other)
    out_v[...] = f_scr[...].astype(BF16)
    out_copy = pltpu.make_async_copy(out_v, out_hbm, out_sem.at[0])
    out_copy.start()
    lse = jnp.concatenate([lbuf[0, :2], lbuf[1, :2]], axis=0)
    hi = lse.astype(BF16)
    rest = lse - hi.astype(F32)
    mid = rest.astype(BF16)
    low = (rest - mid.astype(F32)).astype(BF16)
    lse_v[...] = nn(hi, perm[...]) + nn(mid, perm[...]) + nn(low, perm[...])
    lse_copy = pltpu.make_async_copy(lse_v, lse_hbm, out_sem.at[1])
    lse_copy.start()

    for cp in sends:
        cp.wait_send()
    for half in range(2):
        for dev in range(2):
            fwd_v(dev, half).wait_send()
            fwd_k(dev, half).wait_send()
    o_send.wait_send()
    l_send.wait_send()
    out_copy.wait()
    lse_copy.wait()


def solution(mesh):
    freq = (THETA ** (-(np.arange(64, dtype=np.float64) * 2.0) / D)).astype(np.float32)
    freq = np.broadcast_to(freq[:, None], (64, ROWS)).copy()
    any_spec = pl.BlockSpec(memory_space=pl.ANY)
    dma = pltpu.SemaphoreType.DMA
    vm = pltpu.VMEM

    def per_device(q_raw, k_raw, v_raw, positions, seq_ids, q_gain, k_gain):
        call = pl.pallas_call(
            kernel,
            out_shape=(jax.ShapeDtypeStruct((4 * ROWS, D), BF16), jax.ShapeDtypeStruct((4, ROWS), F32)),
            in_specs=[any_spec] * 8,
            out_specs=(any_spec, any_spec),
            scratch_shapes=[
                vm((4 * ROWS, D), BF16), vm((2 * ROWS, D), BF16), vm((2 * ROWS, D), BF16),
                vm((1, ROWS), jnp.int32), vm((1, ROWS), jnp.int32), vm((1, D), BF16), vm((1, D), BF16),
                vm((64, ROWS), F32),
                vm((4 * ROWS, D), F32), vm((2, 64, ROWS), F32), vm((ROWS, ROWS), BF16), vm((ROWS, ROWS), BF16),
                vm((4, 2, 2, HALF, D), BF16), vm((4, 2, 2, D, HALF), BF16),
                vm((2, 2, HALF, D), BF16), vm((2, 2, D, HALF), BF16),
                vm((2, 2, 2 * D, 2 * HALF), BF16), vm((2, D, 2 * HALF), BF16), vm((HALF, D), BF16),
                vm((2, 2, 1, 2 * HALF), F32), vm((2, 2, 1, 2 * HALF), F32), vm((2, 2, D, 2 * HALF), F32),
                vm((2, D, ROWS), BF16), vm((2, 2, D, ROWS), BF16), vm((8, ROWS), F32), vm((2, 8, ROWS), F32),
                vm((4 * ROWS, D), BF16), vm((4, ROWS), F32),
                dma((8,)), dma((2,)), dma((2, 2, 2)), dma((2, 2, 2)), dma((2, 2)), dma((2,)), dma((2, 2)), dma((2, 2)),
                dma((1,)), dma((1,)), dma((4, 2, 2)), dma((4, 2, 2)), dma((2,)), dma((1,)), dma((1,)),
            ],
            compiler_params=pltpu.CompilerParams(collective_id=0, has_side_effects=True, vmem_limit_bytes=40 * 1024 * 1024),
        )
        out, lse = call(q_raw.reshape(4 * ROWS, D), k_raw.reshape(2 * ROWS, D), v_raw.reshape(2 * ROWS, D),
                        positions.reshape(1, ROWS), seq_ids.reshape(1, ROWS), q_gain.reshape(1, D), k_gain.reshape(1, D),
                        jnp.asarray(freq))
        return out.reshape(ROWS, 4, D), lse.T

    return jax.shard_map(per_device, mesh=mesh, in_specs=(P("cp", "tp", None), P("cp", "tp", None), P("cp", "tp", None), P("cp"), P("cp"), P(), P()), out_specs=(P("cp", "tp", None), P("cp", "tp")), check_vma=False)
```

time: 94.8 us -> 36.6 us (0.39)
  Pallas kernels: 0 us -> 29.7 us
  starting transfers between devices: 28.9 us -> 0 us
  waiting for transfers between devices: 23.7 us -> 0 us
  matrix products: 20.3 us -> 0 us
  other arithmetic: 17.8 us -> 0 us
  local copies, waits for them, and re-layouts: 2.46 us -> 5.91 us
    pallas_call x0 -> x1, Pallas kernels: none -> 29.7 us  [per_device(): call(q_raw.reshape(4 * ROWS, D), k_raw.reshape(2 * ROWS, D), v_raw.reshap...]
    ppermute x28 -> x0, starting transfers between devices: 28.9 us -> none  [the longest x7 20.9 us: body(): v_blk = lax.ppermute(v_blk, 'cp', shift)]
    ppermute x28 -> x0, waiting for transfers between devices: 23.7 us -> none  [the longest x7 19.2 us: body(): k_pos = lax.ppermute(k_pos, 'cp', shift)]
    dot_general x16 -> x0, matrix products: 20.3 us -> none  [the longest x8 13.1 us: key_step(): jnp.einsum('rkgs,skd->rkgd', weights.astype(jnp.bfloat16), v_blk, preferr...]
    reduce_sum x10 -> x0, other arithmetic: 9.16 us -> none  [the longest x8 7.27 us: key_step(): sum_new = sum_run * rescale + jnp.sum(weights, axis=-1)]
    unnamed x12 -> x18, local copies, waits for them, and re-layouts: 0.03 us -> 5.91 us
    convert_element_type x6 -> x0, other arithmetic: 3.59 us -> none  [the longest x2 1.9 us: norm_rope(): (x_f32 * inv_rms * gain.astype(jnp.float32)).astype(jnp.bfloat16)]
    and x8 -> x0, other arithmetic: 2.2 us -> none  [key_step(): (q_seq[:, None] == k_seq[None, :]) & (k_pos[None, :] <= q_pos[:, None])]
  transfers between devices with their start and end apart: 28 -> 0, of which waited for: 14 -> 0; matrix products, arithmetic and copies ran while one was open for 16% -> 0% of each run, Pallas kernels for 0% -> 0%
where the time goes in v1:
time: 36.6 us; the launch traced here: 36.3 us
  Pallas kernels  29.7 us (81%)
  local copies, waits for them, and re-layouts  5.91 us (16%)
  between operations  0.68 us (2%)
    pallas_call x1, Pallas kernels, per_device(): call(q_raw.reshape(4 * ROWS, D), k_raw.reshape(2 * ROWS, D), v_raw.reshap...  29.7 us
    unnamed x18, local copies, waits for them, and re-layouts  5.91 us

profile of v1, /device:TPU:0, one launch (start us, length us, event | category | flops | bytes accessed | tf_op | source)
XLA Modules:
  0.0 36.3 jit_solution(5994425679436800436)
XLA Ops:
  0.6 0.0 copy-start.5
  0.6 0.0 copy-start.4
  0.7 0.0 copy-start.6
  0.7 0.0 copy-start.7
  0.7 0.6 %copy-done.5 = s32[512]{0:T(512)S(1)} copy-done((s32[512]{0:T(512)S(1)}, s32[512]{0:T(512)}, u32[]{:S(2)}) %copy-start.5) | copy-done | bytes 2072
  1.3 0.0 copy-done.4
  1.3 0.0 copy-done.6
  1.3 0.0 copy-done.7
  1.3 0.0 copy-start
  1.3 1.0 %copy-done = bf16[512,4,128]{2,1,0:T(4,128)(2,1)S(1)} copy-done((bf16[512,4,128]{2,1,0:T(4,128)(2,1)S(1)}, bf16[512,4,128]{2,1,0:T(4,128)(2,1)}, u32[]{:S(2)}) %copy-start) | copy-done | bytes 524312
  2.4 0.0 copy-start.1
  2.4 0.9 %copy-done.1 = bf16[512,2,128]{2,1,0:T(2,128)(2,1)S(1)} copy-done((bf16[512,2,128]{2,1,0:T(2,128)(2,1)S(1)}, bf16[512,2,128]{2,1,0:T(2,128)(2,1)}, u32[]{:S(2)}) %copy-start.1) | copy-done | bytes 262168
  3.3 0.0 copy-start.2
  3.3 0.9 %copy-done.2 = bf16[512,2,128]{2,1,0:T(2,128)(2,1)S(1)} copy-done((bf16[512,2,128]{2,1,0:T(2,128)(2,1)S(1)}, bf16[512,2,128]{2,1,0:T(2,128)(2,1)}, u32[]{:S(2)}) %copy-start.2) | copy-done | bytes 262168
  4.3 0.0 copy-start.3
  4.3 0.9 %copy-done.3 = f32[64,512]{1,0:T(8,128)S(1)} copy-done((f32[64,512]{1,0:T(8,128)S(1)}, f32[64,512]{1,0:T(8,128)}, u32[]{:S(2)}) %copy-start.3) | copy-done | bytes 131096
  5.2 29.7 %shard_map.95 = (bf16[2048,128]{1,0:T(8,128)(2,1)S(1)}, f32[4,512]{1,0:T(4,128)S(1)}) custom-call(bf16[2048,128]{1,0:T(8,128)(2,1)S(1)} %bitcast.10, bf16[1024,128]{1,0:T(8,128)(2,1)S(1)} %bitcast.11, bf16[1024,128]{1,0:T(8,128)(2,1)S(1)} %bitcast.12, s32[1,512]{1,0:T(1,128)S(1)} %bitcast.14, s32[1,512]{1,0:T(1,128)S(1)} %bitcast.15, ...), custom_call_target="tpu_custom_call" | custom-call | tf_op jit(solution)/shard_map/pallas_call | solution.py:374
  34.9 0.8 %copy.12 = bf16[512,4,128]{2,1,0:T(4,128)(2,1)} copy(bf16[512,4,128]{2,1,0:T(4,128)(2,1)S(1)} %bitcast.9) | data formatting | bytes 1048576
  35.7 0.6 %copy.13 = f32[512,4]{0,1:T(4,128)} copy(f32[512,4]{0,1:T(4,128)S(1)} %bitcast.13) | data formatting | bytes 16384
Async XLA Ops:
  0.6 0.7 %copy-start.5 = (s32[512]{0:T(512)S(1)}, s32[512]{0:T(512)}, u32[]{:S(2)}) copy-start(s32[512]{0:T(512)} %param.12) | copy-start | bytes 6148
  0.6 0.7 %copy-start.4 = (s32[512]{0:T(512)S(1)}, s32[512]{0:T(512)}, u32[]{:S(2)}) copy-start(s32[512]{0:T(512)} %param.11) | copy-start | bytes 6148
  0.7 0.7 %copy-start.6 = (bf16[128]{0:T(256)(128)(2,1)S(1)}, bf16[128]{0:T(256)(128)(2,1)}, u32[]{:S(2)}) copy-start(bf16[128]{0:T(256)(128)(2,1)} %param.13) | copy-start | bytes 772
  0.7 0.7 %copy-start.7 = (bf16[128]{0:T(256)(128)(2,1)S(1)}, bf16[128]{0:T(256)(128)(2,1)}, u32[]{:S(2)}) copy-start(bf16[128]{0:T(256)(128)(2,1)} %param.14) | copy-start | bytes 772
  1.3 1.0 %copy-start = (bf16[512,4,128]{2,1,0:T(4,128)(2,1)S(1)}, bf16[512,4,128]{2,1,0:T(4,128)(2,1)}, u32[]{:S(2)}) copy-start(bf16[512,4,128]{2,1,0:T(4,128)(2,1)} %param.8) | copy-start | bytes 1572868
  2.4 0.9 %copy-start.1 = (bf16[512,2,128]{2,1,0:T(2,128)(2,1)S(1)}, bf16[512,2,128]{2,1,0:T(2,128)(2,1)}, u32[]{:S(2)}) copy-start(bf16[512,2,128]{2,1,0:T(2,128)(2,1)} %param.9) | copy-start | bytes 786436
  3.3 0.9 %copy-start.2 = (bf16[512,2,128]{2,1,0:T(2,128)(2,1)S(1)}, bf16[512,2,128]{2,1,0:T(2,128)(2,1)}, u32[]{:S(2)}) copy-start(bf16[512,2,128]{2,1,0:T(2,128)(2,1)} %param.10) | copy-start | bytes 786436
  4.3 0.9 %copy-start.3 = (f32[64,512]{1,0:T(8,128)S(1)}, f32[64,512]{1,0:T(8,128)}, u32[]{:S(2)}) copy-start(f32[64,512]{1,0:T(8,128)} %constant.2.clone.freq_hbm) | copy-start | bytes 393220
